TPU v7x, 32 devices: a whole 2x2x4 slice. The times are simulated.
32 devices in a mesh: gz: 8 (over z, y), gy: 4 (over x, core).
Axes of the slice: x: 2, y: 2, z: 4, core: 2. Of those that a mesh axis runs over, the one named last changes fastest.
Arguments:
- right_side: float32 [8, 16, 256, 512], P(None, 'gz', 'gy'), may hold values from -8 to 8
- diagonal: float32 [16, 256, 512], P('gz', 'gy'), may hold values from 0.1 to 4
Outputs:
- solution: float32 [8, 16, 256, 512], P(None, 'gz', 'gy')
- hessenberg: float32 [24, 32], replicated
All inputs are finite; a program needn't handle non-finite values.
Results may differ from a plain program's by a relative error of at most 0.0003.
Values sent between devices are 32-bit elements; how exact they have to be, the bound alone decides.
A program may use at most 64 MiB of HBM per device.

v0:
```python
import jax
import jax.numpy as jnp
from jax import lax
from jax.sharding import PartitionSpec as P

ITERS = 3


def extended(array, sides, width):
    for axis, dim in sides:
        peers, length = (lax.axis_size(axis), array.shape[dim])
        up = [(i, (i + 1) % peers) for i in range(peers - 1)]
        down = [(j, i) for i, j in up]
        last = lax.slice_in_dim(array, length - width, length, axis=dim)
        leading = lax.slice_in_dim(array, 0, width, axis=dim)
        before = lax.ppermute(last, axis, up)
        after = lax.ppermute(leading, axis, down)
        array = jnp.concatenate([before, array, after], axis=dim)
    return array


def stencil(padded, field, diagonal):
    padded = jnp.pad(padded, ((0, 0), (0, 0), (0, 0), (1, 1)))
    beside = padded[:, 2:, 1:-1, 1:-1] + padded[:, :-2, 1:-1, 1:-1]
    beside = beside + padded[:, 1:-1, 2:, 1:-1] + padded[:, 1:-1, :-2, 1:-1]
    beside = beside + padded[:, 1:-1, 1:-1, 2:] + padded[:, 1:-1, 1:-1, :-2]
    return (6.0 + diagonal)[None] * field - beside


def apply_op(field, diagonal):
    padded = extended(field, (("gz", 1), ("gy", 2)), 1)
    return stencil(padded, field, diagonal)


def inner(left, right):
    return jnp.dot(left, right.T, precision=lax.Precision.HIGHEST)


def body(right_side, diagonal):
    shape = right_side.shape
    blocks_n = shape[0]
    flat_rhs = right_side.reshape(blocks_n, -1)
    lower0 = jnp.linalg.cholesky(lax.psum(inner(flat_rhs, flat_rhs), ("gz", "gy")))
    basis = [jax.scipy.linalg.solve_triangular(lower0, flat_rhs, lower=True)]
    rows_out = []
    work = apply_op(basis[0].reshape(shape), diagonal).reshape(blocks_n, -1)
    for step in range(ITERS):
        local = jnp.stack([inner(work, vec) for vec in basis], axis=0)
        coeff, gram_work = lax.psum((local, inner(work, work)), ("gz", "gy"))
        gram = gram_work
        for index in range(step + 1):
            gram = gram - jnp.dot(coeff[index], coeff[index].T, precision=lax.Precision.HIGHEST)
        reduced = work
        for index in range(step + 1):
            reduced = reduced - jnp.dot(coeff[index], basis[index], precision=lax.Precision.HIGHEST)
        more = step + 1 < ITERS
        lower = jnp.linalg.cholesky(gram)
        basis.append(jax.scipy.linalg.solve_triangular(lower, reduced, lower=True))
        if more:
            work = apply_op(basis[-1].reshape(shape), diagonal).reshape(blocks_n, -1)
        pieces = [coeff[index] for index in range(step + 1)]
        pieces = (
            pieces + [lower] + [jnp.zeros((blocks_n, blocks_n), jnp.float32)] * (ITERS - 1 - step)
        )
        rows_out.append(jnp.concatenate(pieces, axis=1))
    hessenberg = jnp.concatenate(rows_out, axis=0)
    normal = jnp.dot(hessenberg, hessenberg.T, precision=lax.Precision.HIGHEST)
    factor = jnp.linalg.cholesky(normal)
    target = jnp.dot(hessenberg[:, :blocks_n], lower0.T, precision=lax.Precision.HIGHEST)
    coeffs = jax.scipy.linalg.cho_solve((factor, True), target)
    stacked = jnp.concatenate(basis[:ITERS], axis=0)
    solution = jnp.dot(coeffs.T, stacked, precision=lax.Precision.HIGHEST)
    return (solution.reshape(shape), hessenberg)


def solution(mesh):
    in_specs = (P(None, "gz", "gy", None), P("gz", "gy", None))
    out_specs = (P(None, "gz", "gy", None), P())
    return jax.shard_map(body, mesh=mesh, in_specs=in_specs, out_specs=out_specs, check_vma=False)
```

profile of v0, /device:TPU:0, one launch (start us, length us, event | category | flops | bytes accessed | tf_op | source)
XLA Modules:
  0.0 452.4 jit_solution(8485363738929407699)
XLA Ops:
  0.6 8.2 %fusion.21 = f32[8,8]{0,1:T(8,128)S(1)} fusion(f32[8,2,64,512]{3,2,1,0:T(8,128)} %param.5), kind=kOutput, calls=%fused_computation.68 | convolution fusion | flops 50331648 | bytes 2097408 | tf_op jit(solution)/shard_map/dot_general | solution.py:36
  8.9 42.0 %psum.49 = f32[8,8]{0,1:T(8,128)S(1)} all-reduce(f32[8,8]{0,1:T(8,128)S(1)} %fusion.21), channel_id=1, replica_groups=mesh['gz'=8,'gy'=4] {'gz','gy'}, use_global_device_ids=true, to_apply=%region_0.0 | all-reduce | flops 64 | bytes 512 | tf_op jit(solution)/shard_map/psum | solution.py:43
  50.9 0.7 cholesky.109
  51.6 0.7 compare_reduce_fusion.3
  52.9 0.6 custom-call.18
  53.5 1.2 copy.39
  54.8 1.9 fusion.36
  56.9 1.3 collective-permute-start
  58.2 5.0 %collective-permute-start.1 = (f32[8,1,64,512]{3,0,2,1:T(8,128)S(1)}, f32[8,1,64,512]{3,0,2,1:T(8,128)S(1)}, u32[]{:S(2)}, u32[]{:S(2)}) collective-permute-start(f32[8,1,64,512]{3,0,2,1:T(8,128)S(1)} %get-tuple-element.26), channel_id=1, source_target_pairs={{0,4},{4,8},{8,12},{12,16},{16,20},{20,24},{24,28},{1,5},{5,9},{9,... | collective-permute-start | bytes 3145736 | tf_op jit(solution)/shard_map/ppermute | solution.py:16
  63.2 19.7 %collective-permute-done = f32[8,1,64,512]{3,0,2,1:T(8,128)S(1)} collective-permute-done((f32[8,1,64,512]{3,0,2,1:T(8,128)S(1)}, f32[8,1,64,512]{3,0,2,1:T(8,128)S(1)}, u32[]{:S(2)}, u32[]{:S(2)}) %collective-permute-start) | collective-permute-done | bytes 1048608 | tf_op jit(solution)/shard_map/ppermute | solution.py:17
  82.9 22.2 %collective-permute-done.1 = f32[8,1,64,512]{3,0,2,1:T(8,128)S(1)} collective-permute-done((f32[8,1,64,512]{3,0,2,1:T(8,128)S(1)}, f32[8,1,64,512]{3,0,2,1:T(8,128)S(1)}, u32[]{:S(2)}, u32[]{:S(2)}) %collective-permute-start.1) | collective-permute-done | bytes 1048608 | tf_op jit(solution)/shard_map/ppermute | solution.py:16
  105.1 1.3 collective-permute-start.2
  106.4 3.2 collective-permute-start.3
  110.3 3.9 select_maximum_fusion.8
  114.2 2.1 fusion.15
  116.3 4.6 %convolution_bitcast_fusion.7 = f32[8,8]{0,1:T(8,128)S(1)} fusion(f32[8,2,64,512]{3,0,2,1:T(8,128)S(1)} %fusion.15), kind=kOutput, calls=%fused_computation.79 | convolution fusion | flops 50331648 | bytes 2097408 | tf_op jit(solution)/shard_map/dot_general | solution.py:36
  120.9 4.9 %fusion.55 = f32[8,8]{1,0:T(8,128)S(1)} fusion(f32[8,65536]{1,0:T(8,128)S(1)} %bitcast.140, f32[8,65536]{1,0:T(8,128)S(1)} %fusion.36), kind=kOutput, calls=%fused_computation.154 | convolution fusion | flops 50331648 | bytes 4194560 | tf_op jit(solution)/shard_map/dot_general | solution.py:36
  125.8 43.6 %all-reduce.5 = (f32[8,8]{1,0:T(8,128)S(1)}, f32[8,8]{0,1:T(8,128)S(1)}) all-reduce(f32[8,8]{1,0:T(8,128)S(1)} %fusion.55, f32[8,8]{0,1:T(8,128)S(1)} %convolution_bitcast_fusion.7), channel_id=1, replica_groups=mesh['gz'=8,'gy'=4] {'gz','gy'}, use_global_device_ids=true, to_apply=%region_3.6 | all-reduce | flops 128 | bytes 1024 | tf_op jit(solution)/shard_map/psum | solution.py:49
  169.5 4.7 %convolution_subtract_fusion.2 = f32[8,65536]{1,0:T(8,128)} fusion(f32[8,65536]{1,0:T(8,128)} %bitcast.141, f32[8,8]{1,0:T(8,128)S(1)} %get-tuple-element.10, f32[8,65536]{1,0:T(8,128)S(1)} %fusion.36), kind=kOutput, calls=%fused_computation.2 | convolution fusion | flops 50855936 | bytes 6291712 | tf_op jit(solution)/shard_map/dot_general | solution.py:55
  174.3 0.7 cholesky.120
  175.1 0.6 compare_reduce_fusion.2
  175.7 0.6 select_bitcast_fusion.1
  177.0 3.5 fusion.34
  180.7 1.3 collective-permute-start.4
  182.0 4.9 %collective-permute-start.5 = (f32[8,1,64,512]{3,0,2,1:T(8,128)S(1)}, f32[8,1,64,512]{3,0,2,1:T(8,128)S(1)}, u32[]{:S(2)}, u32[]{:S(2)}) collective-permute-start(f32[8,1,64,512]{3,0,2,1:T(8,128)S(1)} %get-tuple-element.24), channel_id=1, source_target_pairs={{0,4},{4,8},{8,12},{12,16},{16,20},{20,24},{24,28},{1,5},{5,9},{9,... | collective-permute-start | bytes 3145736 | tf_op jit(solution)/shard_map/ppermute | solution.py:16
  186.9 19.8 %collective-permute-done.4 = f32[8,1,64,512]{3,0,2,1:T(8,128)S(1)} collective-permute-done((f32[8,1,64,512]{3,0,2,1:T(8,128)S(1)}, f32[8,1,64,512]{3,0,2,1:T(8,128)S(1)}, u32[]{:S(2)}, u32[]{:S(2)}) %collective-permute-start.4) | collective-permute-done | bytes 1048608 | tf_op jit(solution)/shard_map/ppermute | solution.py:17
  206.7 21.8 %collective-permute-done.5 = f32[8,1,64,512]{3,0,2,1:T(8,128)S(1)} collective-permute-done((f32[8,1,64,512]{3,0,2,1:T(8,128)S(1)}, f32[8,1,64,512]{3,0,2,1:T(8,128)S(1)}, u32[]{:S(2)}, u32[]{:S(2)}) %collective-permute-start.5) | collective-permute-done | bytes 1048608 | tf_op jit(solution)/shard_map/ppermute | solution.py:16
  228.5 1.3 collective-permute-start.6
  229.8 3.4 collective-permute-start.7
  233.7 3.9 select_maximum_fusion.4
  237.6 2.1 fusion.11
  239.8 4.9 %convolution_bitcast_fusion.6 = f32[1,8,8]{2,1,0:T(8,128)S(1)} fusion(f32[8,65536]{1,0:T(8,128)S(1)} %bitcast.137, f32[8,65536]{1,0:T(8,128)S(1)} %fusion.36), kind=kOutput, calls=%fused_computation.78 | convolution fusion | flops 50331648 | bytes 4194560 | tf_op jit(solution)/shard_map/dot_general | solution.py:36
  244.6 4.9 %convolution_bitcast_fusion.5 = f32[1,8,8]{2,1,0:T(8,128)S(1)} fusion(f32[8,65536]{1,0:T(8,128)S(1)} %bitcast.138, f32[8,65536]{1,0:T(8,128)S(1)} %fusion.34), kind=kOutput, calls=%fused_computation.77 | convolution fusion | flops 50331648 | bytes 4194560 | tf_op jit(solution)/shard_map/dot_general | solution.py:36
  249.6 4.6 %convolution_bitcast_fusion.4 = f32[8,8]{0,1:T(8,128)S(1)} fusion(f32[8,2,64,512]{3,0,2,1:T(8,128)S(1)} %fusion.11), kind=kOutput, calls=%fused_computation.76 | convolution fusion | flops 50331648 | bytes 2097408 | tf_op jit(solution)/shard_map/dot_general | solution.py:36
  254.1 43.2 %all-reduce.4 = (f32[2,8,8]{2,1,0:T(8,128)S(1)}, f32[8,8]{0,1:T(8,128)S(1)}) all-reduce(f32[2,8,8]{2,1,0:T(8,128)S(1)} %pad_maximum_fusion.34, f32[8,8]{0,1:T(8,128)S(1)} %convolution_bitcast_fusion.4), channel_id=1, replica_groups=mesh['gz'=8,'gy'=4] {'gz','gy'}, use_global_device_ids=true, to_apply=%region_5.8 | all-reduce | flops 192 | bytes 1536 | tf_op jit(solution)/shard_map/psum | solution.py:49
  297.4 4.7 %convolution_subtract_fusion.1 = f32[8,65536]{1,0:T(8,128)} fusion(f32[8,65536]{1,0:T(8,128)} %bitcast.139, f32[8,65536]{1,0:T(8,128)S(1)} %fusion.36, f32[2,8,8]{2,1,0:T(8,128)S(1)} %get-tuple-element.8), kind=kOutput, calls=%fused_computation.1 | convolution fusion | flops 50855936 | bytes 6295552 | tf_op jit(solution)/shard_map/dot_general | solution.py:55
  302.4 0.7 cholesky.131
  303.1 0.6 compare_reduce_fusion.1
  303.8 0.6 select_bitcast_fusion
  305.1 4.1 convolution_subtract_fusion
  309.2 2.0 fusion.32
  311.4 1.3 collective-permute-start.8
  312.7 4.9 %collective-permute-start.9 = (f32[8,1,64,512]{3,0,2,1:T(8,128)S(1)}, f32[8,1,64,512]{3,0,2,1:T(8,128)S(1)}, u32[]{:S(2)}, u32[]{:S(2)}) collective-permute-start(f32[8,1,64,512]{3,0,2,1:T(8,128)S(1)} %get-tuple-element.22), channel_id=1, source_target_pairs={{0,4},{4,8},{8,12},{12,16},{16,20},{20,24},{24,28},{1,5},{5,9},{9,... | collective-permute-start | bytes 3145736 | tf_op jit(solution)/shard_map/ppermute | solution.py:16
  317.6 19.8 %collective-permute-done.8 = f32[8,1,64,512]{3,0,2,1:T(8,128)S(1)} collective-permute-done((f32[8,1,64,512]{3,0,2,1:T(8,128)S(1)}, f32[8,1,64,512]{3,0,2,1:T(8,128)S(1)}, u32[]{:S(2)}, u32[]{:S(2)}) %collective-permute-start.8) | collective-permute-done | bytes 1048608 | tf_op jit(solution)/shard_map/ppermute | solution.py:17
  337.3 21.8 %collective-permute-done.9 = f32[8,1,64,512]{3,0,2,1:T(8,128)S(1)} collective-permute-done((f32[8,1,64,512]{3,0,2,1:T(8,128)S(1)}, f32[8,1,64,512]{3,0,2,1:T(8,128)S(1)}, u32[]{:S(2)}, u32[]{:S(2)}) %collective-permute-start.9) | collective-permute-done | bytes 1048608 | tf_op jit(solution)/shard_map/ppermute | solution.py:16
  359.1 1.3 collective-permute-start.10
  360.4 3.0 collective-permute-start.11
  363.5 0.9 collective-permute-done.11
  364.4 3.9 select_maximum_fusion
  368.2 2.3 fusion.7
  370.6 4.9 %convolution_bitcast_fusion.3 = f32[1,8,8]{2,1,0:T(8,128)S(1)} fusion(f32[8,65536]{1,0:T(8,128)S(1)} %bitcast.134, f32[8,65536]{1,0:T(8,128)S(1)} %fusion.36), kind=kOutput, calls=%fused_computation.74 | convolution fusion | flops 50331648 | bytes 4194560 | tf_op jit(solution)/shard_map/dot_general | solution.py:36
  375.5 4.9 %convolution_bitcast_fusion.2 = f32[1,8,8]{2,1,0:T(8,128)S(1)} fusion(f32[8,65536]{1,0:T(8,128)S(1)} %bitcast.135, f32[8,65536]{1,0:T(8,128)S(1)} %copy-done.1), kind=kOutput, calls=%fused_computation.73 | convolution fusion | flops 50331648 | bytes 4194560 | tf_op jit(solution)/shard_map/dot_general | solution.py:36
  380.4 4.9 %convolution_bitcast_fusion.1 = f32[1,8,8]{2,1,0:T(8,128)S(1)} fusion(f32[8,65536]{1,0:T(8,128)S(1)} %bitcast.136, f32[8,65536]{1,0:T(8,128)S(1)} %fusion.32), kind=kOutput, calls=%fused_computation.72 | convolution fusion | flops 50331648 | bytes 4194560 | tf_op jit(solution)/shard_map/dot_general | solution.py:36
  385.3 4.6 %convolution_bitcast_fusion = f32[8,8]{0,1:T(8,128)S(1)} fusion(f32[8,2,64,512]{3,0,2,1:T(8,128)S(1)} %fusion.7), kind=kOutput, calls=%fused_computation.71 | convolution fusion | flops 50331648 | bytes 2097408 | tf_op jit(solution)/shard_map/dot_general | solution.py:36
  389.9 44.3 %all-reduce.3 = (f32[8,8]{0,1:T(8,128)S(1)}, f32[3,8,8]{2,1,0:T(8,128)S(1)}) all-reduce(f32[8,8]{0,1:T(8,128)S(1)} %convolution_bitcast_fusion, f32[3,8,8]{2,1,0:T(8,128)S(1)} %pad_maximum_fusion.33), channel_id=1, replica_groups=mesh['gz'=8,'gy'=4] {'gz','gy'}, use_global_device_ids=true, to_apply=%region_8.11 | all-reduce | flops 256 | bytes 2048 | tf_op jit(solution)/shard_map/psum | solution.py:49
  434.7 0.7 cholesky.142
  435.5 0.6 compare_reduce_fusion
  436.1 0.6 select_select_fusion.1
  437.0 0.8 fusion.25
  437.9 2.2 cholesky.41
  440.1 0.7 compare_reduce_fusion.4
  441.4 1.8 custom-call.15
  443.6 5.9 %fusion = f32[8,65536]{1,0:T(8,128)S(1)} fusion(f32[24,8]{1,0:T(8,128)S(1)} %fusion.27, f32[8,65536]{1,0:T(8,128)} %copy-done.2, f32[8,65536]{1,0:T(8,128)} %copy-done, f32[8,65536]{1,0:T(8,128)S(1)} %fusion.36), kind=kOutput, calls=%fused_computation.5 | convolution fusion | flops 154140672 | bytes 8389376 | tf_op jit(solution)/shard_map/dot_general | solution.py:72
  449.4 2.5 copy.24
  (64 shorter events, 6.2 us)
Async XLA Ops:
  0.6 52.9 %copy-start.5 = (f32[8,2,64,512]{3,2,1,0:T(8,128)S(1)}, f32[8,2,64,512]{3,2,1,0:T(8,128)}, u32[]{:S(2)}) copy-start(f32[8,2,64,512]{3,2,1,0:T(8,128)} %param.5) | copy-start | bytes 6291460
  56.9 26.0 %collective-permute-start = (f32[8,1,64,512]{3,0,2,1:T(8,128)S(1)}, f32[8,1,64,512]{3,0,2,1:T(8,128)S(1)}, u32[]{:S(2)}, u32[]{:S(2)}) collective-permute-start(f32[8,1,64,512]{3,0,2,1:T(8,128)S(1)} %get-tuple-element.27), channel_id=1, source_target_pairs={{4,0},{8,4},{12,8},{16,12},{20,16},{24,20},{28,24},{5,1},{9,5},{13... | collective-permute-start | bytes 3145736 | tf_op jit(solution)/shard_map/ppermute | solution.py:17
  58.2 51.5 %copy-start.6 = (f32[2,64,512]{2,1,0:T(8,128)S(1)}, f32[2,64,512]{2,1,0:T(8,128)}, u32[]{:S(2)}) copy-start(f32[2,64,512]{2,1,0:T(8,128)} %param.6) | copy-start | bytes 786436
  58.2 46.9 %collective-permute-start.1 = (f32[8,1,64,512]{3,0,2,1:T(8,128)S(1)}, f32[8,1,64,512]{3,0,2,1:T(8,128)S(1)}, u32[]{:S(2)}, u32[]{:S(2)}) collective-permute-start(f32[8,1,64,512]{3,0,2,1:T(8,128)S(1)} %get-tuple-element.26), channel_id=1, source_target_pairs={{0,4},{4,8},{8,12},{12,16},{16,20},{20,24},{24,28},{1,5},{5,9},{9,... | collective-permute-start | bytes 3145736 | tf_op jit(solution)/shard_map/ppermute | solution.py:16
  105.1 4.6 %collective-permute-start.2 = (f32[8,4,1,512]{3,0,2,1:T(8,128)S(1)}, f32[8,4,1,512]{3,0,2,1:T(8,128)S(1)}, u32[]{:S(2)}, u32[]{:S(2)}) collective-permute-start(f32[8,4,1,512]{3,0,2,1:T(8,128)S(1)} %get-tuple-element.21), channel_id=1, source_target_pairs={{1,0},{2,1},{3,2},{5,4},{6,5},{7,6},{9,8},{10,9},{11,10},{13,12},{... | collective-permute-start | bytes 196616 | tf_op jit(solution)/shard_map/ppermute | solution.py:17
  106.4 3.9 collective-permute-start.3
  116.3 4.6 %copy-start.4 = (f32[8,2,64,512]{3,0,2,1:T(8,128)}, f32[8,2,64,512]{3,0,2,1:T(8,128)S(1)}, u32[]{:S(2)}) copy-start(f32[8,2,64,512]{3,0,2,1:T(8,128)S(1)} %fusion.15) | copy-start | bytes 6291460
  180.5 64.1 %copy-start = (f32[8,65536]{1,0:T(8,128)}, f32[8,65536]{1,0:T(8,128)S(1)}, u32[]{:S(2)}) copy-start(f32[8,65536]{1,0:T(8,128)S(1)} %fusion.34) | copy-start | bytes 6291460
  180.7 26.0 %collective-permute-start.4 = (f32[8,1,64,512]{3,0,2,1:T(8,128)S(1)}, f32[8,1,64,512]{3,0,2,1:T(8,128)S(1)}, u32[]{:S(2)}, u32[]{:S(2)}) collective-permute-start(f32[8,1,64,512]{3,0,2,1:T(8,128)S(1)} %get-tuple-element.25), channel_id=1, source_target_pairs={{4,0},{8,4},{12,8},{16,12},{20,16},{24,20},{28,24},{5,1},{9,5},{13... | collective-permute-start | bytes 3145736 | tf_op jit(solution)/shard_map/ppermute | solution.py:17
  182.0 46.5 %collective-permute-start.5 = (f32[8,1,64,512]{3,0,2,1:T(8,128)S(1)}, f32[8,1,64,512]{3,0,2,1:T(8,128)S(1)}, u32[]{:S(2)}, u32[]{:S(2)}) collective-permute-start(f32[8,1,64,512]{3,0,2,1:T(8,128)S(1)} %get-tuple-element.24), channel_id=1, source_target_pairs={{0,4},{4,8},{8,12},{12,16},{16,20},{20,24},{24,28},{1,5},{5,9},{9,... | collective-permute-start | bytes 3145736 | tf_op jit(solution)/shard_map/ppermute | solution.py:16
  228.5 4.7 %collective-permute-start.6 = (f32[8,4,1,512]{3,0,2,1:T(8,128)S(1)}, f32[8,4,1,512]{3,0,2,1:T(8,128)S(1)}, u32[]{:S(2)}, u32[]{:S(2)}) collective-permute-start(f32[8,4,1,512]{3,0,2,1:T(8,128)S(1)} %get-tuple-element.19), channel_id=1, source_target_pairs={{1,0},{2,1},{3,2},{5,4},{6,5},{7,6},{9,8},{10,9},{11,10},{13,12},{... | collective-permute-start | bytes 196616 | tf_op jit(solution)/shard_map/ppermute | solution.py:17
  229.8 3.9 collective-permute-start.7
  239.8 9.8 %copy-start.3 = (f32[8,2,64,512]{3,0,2,1:T(8,128)}, f32[8,2,64,512]{3,0,2,1:T(8,128)S(1)}, u32[]{:S(2)}) copy-start(f32[8,2,64,512]{3,0,2,1:T(8,128)S(1)} %fusion.11) | copy-start | bytes 6291460
  311.2 69.2 %copy-start.2 = (f32[8,65536]{1,0:T(8,128)}, f32[8,65536]{1,0:T(8,128)S(1)}, u32[]{:S(2)}) copy-start(f32[8,65536]{1,0:T(8,128)S(1)} %fusion.32) | copy-start | bytes 6291460
  311.4 26.0 %collective-permute-start.8 = (f32[8,1,64,512]{3,0,2,1:T(8,128)S(1)}, f32[8,1,64,512]{3,0,2,1:T(8,128)S(1)}, u32[]{:S(2)}, u32[]{:S(2)}) collective-permute-start(f32[8,1,64,512]{3,0,2,1:T(8,128)S(1)} %get-tuple-element.23), channel_id=1, source_target_pairs={{4,0},{8,4},{12,8},{16,12},{20,16},{24,20},{28,24},{5,1},{9,5},{13... | collective-permute-start | bytes 3145736 | tf_op jit(solution)/shard_map/ppermute | solution.py:17
  312.7 46.5 %collective-permute-start.9 = (f32[8,1,64,512]{3,0,2,1:T(8,128)S(1)}, f32[8,1,64,512]{3,0,2,1:T(8,128)S(1)}, u32[]{:S(2)}, u32[]{:S(2)}) collective-permute-start(f32[8,1,64,512]{3,0,2,1:T(8,128)S(1)} %get-tuple-element.22), channel_id=1, source_target_pairs={{0,4},{4,8},{8,12},{12,16},{16,20},{20,24},{24,28},{1,5},{5,9},{9,... | collective-permute-start | bytes 3145736 | tf_op jit(solution)/shard_map/ppermute | solution.py:16
  359.1 4.4 collective-permute-start.10
  360.4 3.9 collective-permute-start.11
  370.6 4.9 %copy-start.1 = (f32[8,65536]{1,0:T(8,128)S(1)}, f32[8,65536]{1,0:T(8,128)}, u32[]{:S(2)}) copy-start(f32[8,65536]{1,0:T(8,128)} %copy-done) | copy-start | bytes 6291460
  436.9 12.6 %copy-start.7 = (f32[24,32]{1,0:T(8,128)}, f32[24,32]{1,0:T(8,128)S(1)}, u32[]{:S(2)}) copy-start(f32[24,32]{1,0:T(8,128)S(1)} %maximum_maximum_fusion) | copy-start | bytes 9220
where the time goes:
time: 461 us; the launch traced here: 452 us
  blocking collectives  173 us (38%)
  waiting for transfers between devices  127 us (28%)
  matrix products  80.2 us (17%)
  other arithmetic  33.7 us (7%)
  starting transfers between devices  32.2 us (7%)
  local copies, waits for them, and re-layouts  4.69 us (1%)
    psum x3, blocking collectives, body(): coeff, gram_work = lax.psum((local, inner(work, work)), ('gz', 'gy'))  131 us
    ppermute x6, waiting for transfers between devices, extended(): before = lax.ppermute(last, axis, up)  67.8 us
    ppermute x6, waiting for transfers between devices, extended(): after = lax.ppermute(leading, axis, down)  59.2 us
    dot_general x10, matrix products, inner(): return jnp.dot(left, right.T, precision=lax.Precision.HIGHEST)  51.3 us
    psum x1, blocking collectives, body(): lax.psum(inner(flat_rhs, flat_rhs), ('gz', 'gy'))  42 us
    ppermute x6, starting transfers between devices, extended(): before = lax.ppermute(last, axis, up)  24.5 us
    dot_general x3, matrix products, body(): jnp.dot(coeff[index], basis[index], precision=lax.Precision.HIGHEST)  13.6 us
    concatenate x6, other arithmetic, extended(): array = jnp.concatenate([before, array, after], axis=dim)  11.6 us
  transfers between devices with their start and end apart: 12, of which 9 were waited for; matrix products, arithmetic and copies ran while one was open for 0% of the time, Pallas kernels for 0%

commit v1 on v0

v1 whole, which is shorter than its diff:
```python
import functools

import jax
import jax.numpy as jnp
from jax import lax
from jax.experimental import pallas as pl
from jax.experimental.pallas import tpu as pltpu
from jax.sharding import PartitionSpec as P

ITERS = 3
CENTRE = 7.5
SCALE = 0.25
CHUNKS = 4
MESH = pl.DeviceIdType.MESH
HIGH = lax.Precision.HIGHEST


def nt_dot(left, right):
    return lax.dot_general(
        left, right, (((1,), (1,)), ((), ())), precision=HIGH, preferred_element_type=jnp.float32
    )


def dot(left, right):
    return jnp.dot(left, right, precision=HIGH, preferred_element_type=jnp.float32)


def kernel(
    r_ref, d_ref, out_ref, hess_ref,
    k0, k1, k2, k3, diag, ret1, ret2, ys, yh, acc, mine, slots1, part, slots2, splat,
    x_s, x_r, d_s, d_r, z_s, z_r, y_s, y_r, b_s, b_r, g1_s, g1_r, g2_s, g2_r,
):
    blk, lay, rows, nx = r_ref.shape
    half, group_lay = rows // 2, 2 * lay
    vc = blk // CHUNKS
    n_z, n_y = lax.axis_size("gz"), lax.axis_size("gy")
    gz, gy = lax.axis_index("gz"), lax.axis_index("gy")
    p, group = gz % 2, gz // 2
    h = (p + gy) % 2
    partner = gz + 1 - 2 * p
    hs = pl.multiple_of(h * half, half)
    os = pl.multiple_of((1 - h) * half, half)
    mine_at = p * lay
    theirs_at = (1 - p) * lay
    below, above = group > 0, group < n_z // 2 - 1
    place = 2 * gy + h
    before, after = place > 0, place < 2 * n_y - 1
    prev_dev = (gz + h * (partner - gz), gy - (1 - h))
    next_dev = (gz + (1 - h) * (partner - gz), gy + h)
    basis = (k0, k1, k2, k3)
    edge = (lay - 1) * p

    def remote(src, dst, send, recv, dev):
        return pltpu.make_async_remote_copy(
            src_ref=src, dst_ref=dst, send_sem=send, recv_sem=recv, device_id=dev,
            device_id_type=MESH,
        )

    @pl.when(jnp.logical_not(below))
    def _():
        for k in (k0, k1, k2):
            k[:, 0] = jnp.zeros((blk, half, nx), jnp.float32)

    @pl.when(jnp.logical_not(above))
    def _():
        for k in (k0, k1, k2):
            k[:, group_lay + 1] = jnp.zeros((blk, half, nx), jnp.float32)

    @pl.when(jnp.logical_not(before))
    def _():
        yh[:, 0] = jnp.zeros((ITERS,) + yh.shape[2:], jnp.float32)

    @pl.when(jnp.logical_not(after))
    def _():
        yh[:, 1] = jnp.zeros((ITERS,) + yh.shape[2:], jnp.float32)

    barrier = pltpu.get_barrier_semaphore()
    for step in range(1, n_z):
        pl.semaphore_signal(
            barrier, inc=1, device_id=((gz + step) % n_z, gy), device_id_type=MESH
        )
    for step in range(1, n_y):
        pl.semaphore_signal(
            barrier, inc=1, device_id=(gz, (gy + step) % n_y), device_id_type=MESH
        )
    pl.semaphore_wait(barrier, n_z + n_y - 2)

    def exchange(which, ch):
        layer = edge + which * (1 - 2 * p)
        vs = pl.ds(ch * vc, vc)
        return remote(
            r_ref.at[vs, pl.ds(layer, 1), pl.ds(os, half)],
            k0.at[vs, pl.ds(1 + mine_at + layer, 1)],
            x_s.at[which, ch], x_r.at[which, ch], (partner, gy),
        )

    def z_from_rhs(ch, direction):
        vs = pl.ds(ch * vc, vc)
        if direction == 0:
            dst, dev = k0.at[vs, pl.ds(group_lay + 1, 1)], (gz - 2, gy)
        else:
            dst, dev = k0.at[vs, pl.ds(0, 1)], (gz + 2, gy)
        return remote(
            r_ref.at[vs, pl.ds(edge, 1), pl.ds(hs, half)], dst,
            z_s.at[0, direction, ch], z_r.at[0, direction, ch], dev,
        )

    def z_copy(j, ch, direction):
        vs = pl.ds(ch * vc, vc)
        k = basis[j]
        if direction == 0:
            src, dst, dev = k.at[vs, pl.ds(1, 1)], k.at[vs, pl.ds(group_lay + 1, 1)], (gz - 2, gy)
        else:
            src, dst, dev = k.at[vs, pl.ds(group_lay, 1)], k.at[vs, pl.ds(0, 1)], (gz + 2, gy)
        return remote(src, dst, z_s.at[j, direction, ch], z_r.at[j, direction, ch], dev)

    def y_copy(j, ch, side):
        vs = pl.ds(ch * vc, vc)
        dev = prev_dev if side == 0 else next_dev
        return remote(
            ys.at[j, side, vs], yh.at[j, 1 - side, vs],
            y_s.at[j, side, ch], y_r.at[j, 1 - side, ch], dev,
        )

    def y_wait_recv(j, ch, side):
        vs = pl.ds(ch * vc, vc)
        remote(
            ys.at[j, side, vs], yh.at[j, side, vs], y_s.at[j, side, ch], y_r.at[j, side, ch],
            (partner, gy),
        ).wait_recv()

    def back_copy(j, ch):
        vs = pl.ds(ch * vc, vc)
        dst = (ret1, ret2)[j - 1]
        return remote(
            basis[j].at[vs, pl.ds(1 + theirs_at, lay)], dst.at[vs],
            b_s.at[j - 1, ch], b_r.at[j - 1, ch], (partner, gy),
        )

    diag_copy = remote(
        d_ref.at[:, pl.ds(os, half)], diag.at[pl.ds(mine_at, lay)], d_s, d_r, (partner, gy)
    )

    def chunks(body):
        def run(ch, carry):
            body(ch)
            return carry

        lax.fori_loop(0, CHUNKS, run, 0)

    def first(ch):
        exchange(0, ch).start()

        @pl.when((p == 0) & below)
        def _():
            z_from_rhs(ch, 0).start()

        @pl.when((p == 1) & above)
        def _():
            z_from_rhs(ch, 1).start()

    chunks(first)
    chunks(lambda ch: exchange(1, ch).start())
    diag_copy.start()

    def own(v, carry):
        k0[v, pl.ds(1 + mine_at, lay)] = r_ref[v, :, pl.ds(hs, half)]
        return carry

    lax.fori_loop(0, blk, own, 0)
    diag[pl.ds(mine_at, lay)] = d_ref[:, pl.ds(hs, half)]

    lanes = nx // 128

    def gram(moment, left, right, l_at, r_at, layers, height):
        tiles = height // 8
        pairs = [(a, b) for a in range(blk) for b in range(a, blk)]

        def run(i, sums):
            layer, at = i // tiles, pl.multiple_of((i % tiles) * 8, 8)
            for lane in range(lanes):
                cols = pl.ds(lane * 128, 128)
                x = [left[v, l_at + layer, pl.ds(at, 8), cols] for v in range(blk)]
                y = x if left is right else [
                    right[v, r_at + layer, pl.ds(at, 8), cols] for v in range(blk)
                ]
                sums = tuple(s + x[a] * y[b] for s, (a, b) in zip(sums, pairs))
            return sums

        zero = jnp.zeros((8, 128), jnp.float32)
        sums = lax.fori_loop(0, layers * tiles, run, (zero,) * len(pairs))
        for s, (a, b) in zip(sums, pairs):
            line = jnp.sum(s, axis=0, keepdims=True)
            at = (moment * blk + a) * blk + b
            acc[at:at + 1] = line
            if a != b:
                at = (moment * blk + b) * blk + a
                acc[at:at + 1] = line

    acc[7 * blk * blk:] = jnp.zeros((acc.shape[0] - 7 * blk * blk, 128), jnp.float32)
    gram(0, r_ref, r_ref, 0, 0, lay, rows)

    def relay(ch):
        exchange_in = remote(
            r_ref.at[pl.ds(0, vc), pl.ds(0, 1), pl.ds(os, half)],
            k0.at[pl.ds(ch * vc, vc), pl.ds(1 + (group_lay - 1) * (1 - p), 1)],
            x_s.at[0, ch], x_r.at[0, ch], (partner, gy),
        )
        exchange_in.wait_recv()

        @pl.when((p == 0) & above)
        def _():
            z_copy(0, ch, 1).start()

        @pl.when((p == 1) & below)
        def _():
            z_copy(0, ch, 0).start()

    chunks(relay)

    def stage_rows(j, v, layer, value):
        ys[j, 0, v, layer:layer + 1] = value[:1]
        ys[j, 1, v, layer:layer + 1] = value[half - 1:]

    def start_rows(j, ch):
        @pl.when(before)
        def _():
            y_copy(j, ch, 0).start()

        @pl.when(after)
        def _():
            y_copy(j, ch, 1).start()

    def arrived(ch):
        remote(
            r_ref.at[pl.ds(0, vc), pl.ds(0, 1), pl.ds(os, half)],
            k0.at[pl.ds(ch * vc, vc), pl.ds(1 + lay - p, 1)],
            x_s.at[1, ch], x_r.at[1, ch], (partner, gy),
        ).wait_recv()

        def run(v, carry):
            for layer in range(group_lay):
                stage_rows(0, v, layer, k0[v, 1 + layer])
            return carry

        lax.fori_loop(ch * vc, (ch + 1) * vc, run, 0)
        start_rows(0, ch)

    chunks(arrived)
    remote(
        d_ref.at[:, pl.ds(os, half)], diag.at[pl.ds(theirs_at, lay)], d_s, d_r, (partner, gy)
    ).wait_recv()

    row_at = lax.broadcasted_iota(jnp.int32, (half, nx), 0)
    col_at = lax.broadcasted_iota(jnp.int32, (half, nx), 1)

    def step(j):
        src, dst = basis[j], basis[j + 1]
        shift = 0 if j == 2 else 1

        def apply(ch):
            @pl.when(below)
            def _():
                vs = pl.ds(ch * vc, vc)
                remote(
                    src.at[vs, pl.ds(1, 1)], src.at[vs, pl.ds(0, 1)],
                    z_s.at[j, 1, ch], z_r.at[j, 1, ch], (partner, gy),
                ).wait_recv()

            @pl.when(above)
            def _():
                vs = pl.ds(ch * vc, vc)
                remote(
                    src.at[vs, pl.ds(1, 1)], src.at[vs, pl.ds(group_lay + 1, 1)],
                    z_s.at[j, 0, ch], z_r.at[j, 0, ch], (partner, gy),
                ).wait_recv()

            @pl.when(before)
            def _():
                y_wait_recv(j, ch, 0)

            @pl.when(after)
            def _():
                y_wait_recv(j, ch, 1)

            def run(v, carry):
                for layer in range(group_lay):
                    here = src[v, 1 + layer]
                    near = src[v, layer] + src[v, 2 + layer]
                    up = jnp.where(
                        row_at == 0, yh[j, 0, v, layer:layer + 1], pltpu.roll(here, 1, 0)
                    )
                    down = jnp.where(
                        row_at == half - 1, yh[j, 1, v, layer:layer + 1],
                        pltpu.roll(here, half - 1, 0),
                    )
                    left = jnp.where(col_at == 0, 0.0, pltpu.roll(here, 1, 1))
                    right = jnp.where(col_at == nx - 1, 0.0, pltpu.roll(here, nx - 1, 1))
                    near = near + (up + down) + (left + right)
                    centre = (6.0 - CENTRE) + diag[layer]
                    value = SCALE * (centre * here - near)
                    dst[v, shift + layer] = value
                    if j < 2:
                        stage_rows(j + 1, v, layer, value)
                return carry

            lax.fori_loop(ch * vc, (ch + 1) * vc, run, 0)
            if j < 2:
                @pl.when(below)
                def _():
                    z_copy(j + 1, ch, 0).start()

                @pl.when(above)
                def _():
                    z_copy(j + 1, ch, 1).start()

                start_rows(j + 1, ch)
                back_copy(j + 1, ch).start()

        chunks(apply)
        gram(2 * j + 1, src, dst, 1, shift, group_lay, half)
        gram(2 * j + 2, dst, dst, shift, shift, group_lay, half)

    for j in range(ITERS):
        step(j)

    count = acc.shape[0]
    sums = nt_dot(jnp.ones((8, 128), jnp.float32), acc[...])
    lane_q = lax.broadcasted_iota(jnp.int32, (8, count), 1)
    row_q = lax.broadcasted_iota(jnp.int32, (8, count), 0)
    q = lax.broadcasted_iota(jnp.int32, (count, 128), 0)
    c = lax.broadcasted_iota(jnp.int32, (count, 128), 1)
    pick = (q // (blk * blk) == c // blk) & (q % blk == c % blk)
    kept = jnp.where((lane_q // blk) % blk == row_q, sums, 0.0)
    local = dot(kept, jnp.where(pick, 1.0, 0.0))
    mine[...] = local
    slots1[gy] = local

    def along(n, me, src, slots, send, recv, axis):
        at = (lambda i: (gz, i)) if axis == "gy" else (lambda i: (i, gy))
        for off in range(1, n):
            to = (me + off) % n
            remote(src, slots.at[me], send.at[to], recv.at[me], at(to)).start()
        for off in range(1, n):
            frm = (me + off) % n
            remote(src, slots.at[frm], send.at[frm], recv.at[frm], at(frm)).wait()
        total = slots[0]
        for i in range(1, n):
            total = total + slots[i]
        return total

    summed = along(n_y, gy, mine, slots1, g1_s, g1_r, "gy")
    part[...] = summed
    slots2[gz] = summed
    moments = along(n_z, gz, part, slots2, g2_s, g2_r, "gz")

    lane = lax.broadcasted_iota(jnp.int32, (8, 128), 1)
    keep = lambda x, low, high: jnp.where((lane >= low) & (lane < high), x, 0.0)
    left_by = lambda x, n: x if n == 0 else pltpu.roll(x, 128 - n, 1)
    order = (ITERS + 1) * blk
    lane32 = lax.broadcasted_iota(jnp.int32, (order, 128), 1)
    row32 = lax.broadcasted_iota(jnp.int32, (order, 128), 0)
    full = jnp.concatenate(
        [keep(left_by(moments, blk * i), 0, order) for i in range(ITERS + 1)], axis=0
    )
    full = full + jnp.where(lane32 == row32 + order, 1.0, 0.0)
    inv = 1.0 / SCALE
    second = (
        (inv * inv) * left_by(moments, 2 * blk)
        + (2.0 * CENTRE * inv) * left_by(moments, blk)
        + (CENTRE * CENTRE) * moments
    )
    target = inv * left_by(moments, blk) + CENTRE * moments
    small = ITERS * blk
    normal = jnp.concatenate(
        [
            keep(left_by(second, blk * i), 0, small)
            + keep(pltpu.roll(target, small - blk * i, 1) if i < ITERS else target, small, order)
            for i in range(ITERS)
        ],
        axis=0,
    )
    rows_small = lax.broadcasted_iota(jnp.int32, (small, 1), 0)
    rows_full = lax.broadcasted_iota(jnp.int32, (order, 1), 0)
    for k in range(order):
        if k < small:
            row = normal[k:k + 1] / normal[k:k + 1, k:k + 1]
            column = jnp.where(rows_small == k, 0.0, normal[:, k:k + 1])
            normal = jnp.where(rows_small == k, row, normal - column * row)
        row = full[k:k + 1] / full[k:k + 1, k:k + 1]
        column = jnp.where(rows_full <= k, 0.0, full[:, k:k + 1])
        full = full - column * row
    pivots = jnp.sum(jnp.where(lane32 == row32, full, 0.0), axis=1, keepdims=True)
    full = full / jnp.sqrt(pivots)
    upper = jnp.where((lane32 < order) & (lane32 >= row32), full, 0.0)
    lower_inv = left_by(full, order)
    lower_inv = jnp.where(lane32 < small, lower_inv, 0.0)[:small]
    hess = inv * nt_dot(pltpu.roll(lower_inv, blk, 1), upper)
    eye = lax.broadcasted_iota(jnp.int32, (small, order), 0) == lax.broadcasted_iota(
        jnp.int32, (small, order), 1
    )
    row_b = lax.broadcasted_iota(jnp.int32, (small, order), 0) // blk
    col_b = lax.broadcasted_iota(jnp.int32, (small, order), 1) // blk
    hess = hess + jnp.where(eye, CENTRE, 0.0)
    hess_ref[...] = jnp.where(col_b <= row_b + 1, hess, 0.0)

    for k in range(small):
        for u in range(blk):
            splat[k * blk + u] = jnp.broadcast_to(
                normal[k:k + 1, small + u:small + u + 1], (8, 128)
            )

    tiles = half // 8

    def combine(row_start, sources):
        def run(i, carry):
            layer, t = i // tiles, i % tiles
            at = pl.multiple_of(row_start + t * 8, 8)
            for lane_at in range(lanes):
                cols = pl.ds(lane_at * 128, 128)
                vals = []
                for ref, l_at, base in sources:
                    first_row = pl.multiple_of(base + t * 8, 8)
                    vals += [ref[v, l_at + layer, pl.ds(first_row, 8), cols] for v in range(blk)]
                for u in range(blk):
                    total = splat[u] * vals[0]
                    for k in range(1, small):
                        total = total + splat[k * blk + u] * vals[k]
                    out_ref[u, layer, pl.ds(at, 8), cols] = total
            return carry

        lax.fori_loop(0, lay * tiles, run, 0)

    combine(hs, ((r_ref, 0, hs), (k1, 1 + mine_at, 0), (k2, 1 + mine_at, 0)))

    def back_wait(ch):
        for j in (1, 2):
            back_copy(j, ch).wait()

    chunks(back_wait)
    combine(os, ((r_ref, 0, os), (ret1, 0, 0), (ret2, 0, 0)))

    def drain(ch):
        for which in (0, 1):
            exchange(which, ch).wait_send()
        for j in range(ITERS):
            @pl.when(below)
            def _():
                z_copy(j, ch, 0).wait_send()

            @pl.when(above)
            def _():
                z_copy(j, ch, 1).wait_send()

            @pl.when(before)
            def _():
                y_copy(j, ch, 0).wait_send()

            @pl.when(after)
            def _():
                y_copy(j, ch, 1).wait_send()

    chunks(drain)
    diag_copy.wait_send()


def body(right_side, diagonal):
    blk, lay, rows, nx = right_side.shape
    half, group_lay = rows // 2, 2 * lay
    n_z, n_y = lax.axis_size("gz"), lax.axis_size("gy")
    vmem = lambda *shape: pltpu.VMEM(shape, jnp.float32)
    dma = lambda *shape: pltpu.SemaphoreType.DMA(shape)
    small, order = ITERS * blk, (ITERS + 1) * blk
    return pl.pallas_call(
        kernel,
        out_shape=(
            jax.ShapeDtypeStruct(right_side.shape, jnp.float32),
            jax.ShapeDtypeStruct((small, order), jnp.float32),
        ),
        in_specs=[pl.BlockSpec(memory_space=pltpu.VMEM)] * 2,
        out_specs=(pl.BlockSpec(memory_space=pltpu.VMEM),) * 2,
        scratch_shapes=[
            vmem(blk, group_lay + 2, half, nx),
            vmem(blk, group_lay + 2, half, nx),
            vmem(blk, group_lay + 2, half, nx),
            vmem(blk, group_lay, half, nx),
            vmem(group_lay, half, nx),
            vmem(blk, lay, half, nx),
            vmem(blk, lay, half, nx),
            vmem(ITERS, 2, blk, group_lay, nx),
            vmem(ITERS, 2, blk, group_lay, nx),
            vmem(8 * blk * blk, 128),
            vmem(8, 128),
            vmem(n_y, 8, 128),
            vmem(8, 128),
            vmem(n_z, 8, 128),
            vmem(small * blk, 8, 128),
            dma(2, CHUNKS), dma(2, CHUNKS),
            pltpu.SemaphoreType.DMA, pltpu.SemaphoreType.DMA,
            dma(ITERS, 2, CHUNKS), dma(ITERS, 2, CHUNKS),
            dma(ITERS, 2, CHUNKS), dma(ITERS, 2, CHUNKS),
            dma(2, CHUNKS), dma(2, CHUNKS),
            dma(n_y), dma(n_y), dma(n_z), dma(n_z),
        ],
        compiler_params=pltpu.CompilerParams(
            collective_id=0, has_side_effects=True, vmem_limit_bytes=60 * 1024 * 1024
        ),
        name="gmres",
    )(right_side, diagonal)


def solution(mesh):
    in_specs = (P(None, "gz", "gy", None), P("gz", "gy", None))
    out_specs = (P(None, "gz", "gy", None), P())
    return jax.shard_map(body, mesh=mesh, in_specs=in_specs, out_specs=out_specs, check_vma=False)
```

time: 461 us -> 104 us (0.23); the launches traced: 452 us -> 104 us
  blocking collectives: 173 us -> 0 us
  waiting for transfers between devices: 127 us -> 0 us
  Pallas kernels: 0 us -> 99.5 us
  matrix products: 80.2 us -> 0 us
  other arithmetic: 33.7 us -> 0 us
  starting transfers between devices: 32.2 us -> 0 us
    psum x4 -> x0, blocking collectives: 173 us -> none  [the longest x3 131 us: body(): coeff, gram_work = lax.psum((local, inner(work, work)), ('gz', 'gy'))]
    ppermute x12 -> x0, waiting for transfers between devices: 127 us -> none  [the longest x6 67.8 us: extended(): before = lax.ppermute(last, axis, up)]
    pallas_call x0 -> x1, Pallas kernels: none -> 99.5 us  [body(): pl.pallas_call(kernel, out_shape=(jax.ShapeDtypeStruct(right_side.shape,...]
    dot_general x22 -> x0, matrix products: 72.4 us -> none  [the longest x10 51.3 us: inner(): return jnp.dot(left, right.T, precision=lax.Precision.HIGHEST)]
    ppermute x12 -> x0, starting transfers between devices: 32.2 us -> none  [the longest x6 24.5 us: extended(): before = lax.ppermute(last, axis, up)]
    another operation x25 -> x0, other arithmetic: 14.7 us -> none  [the longest x9 4.2 us: body(): lower = jnp.linalg.cholesky(gram)]
    concatenate x7 -> x0, other arithmetic: 11.7 us -> none  [the longest x6 11.6 us: extended(): array = jnp.concatenate([before, array, after], axis=dim)]
    another operation x5 -> x0, matrix products: 7.78 us -> none  [the longest x2 5.51 us: body(): basis.append(jax.scipy.linalg.solve_triangular(lower, reduced, lower=True))]
  transfers between devices with their start and end apart: 12 -> 0, of which waited for: 9 -> 0; matrix products, arithmetic and copies ran while one was open for 0% -> 0% of each run, Pallas kernels for 0% -> 0%
where the time goes in v1:
time: 104 us
  Pallas kernels  99.5 us (96%)
  local copies, waits for them, and re-layouts  3.75 us (4%)
    pallas_call x1, Pallas kernels, body(): pl.pallas_call(kernel, out_shape=(jax.ShapeDtypeStruct(right_side.shape,...  99.5 us
    unnamed x4, local copies, waits for them, and re-layouts  3.75 us

profile of v1, /device:TPU:0, one launch (start us, length us, event | category | flops | bytes accessed | tf_op | source)
XLA Modules:
  0.0 103.9 jit_solution(4251301957684176635)
XLA Ops:
  0.6 99.5 %gmres.1 = (f32[8,2,64,512]{3,2,1,0:T(8,128)}, f32[24,32]{1,0:T(8,128)}) custom-call(f32[8,2,64,512]{3,2,1,0:T(8,128)} %r_ref.1, f32[2,64,512]{2,1,0:T(8,128)} %d_ref.1), custom_call_target="tpu_custom_call" | custom-call | tf_op jit(solution)/shard_map/gmres/pallas_call | solution.py:474
  100.1 0.0 copy-start
  100.1 3.1 %copy.6 = f32[8,2,64,512]{3,2,1,0:T(8,128)} copy(f32[8,2,64,512]{3,2,1,0:T(8,128)} %get-tuple-element.4) | data formatting | bytes 4194304
  103.3 0.0 copy-done
  103.3 0.6 copy.7
Async XLA Ops:
  100.1 3.2 %copy-start = (f32[24,32]{1,0:T(8,128)S(1)}, f32[24,32]{1,0:T(8,128)}, u32[]{:S(2)}) copy-start(f32[24,32]{1,0:T(8,128)} %get-tuple-element.5) | copy-start | bytes 9220

commit v2 on v1

--- a/solution.py
+++ b/solution.py
@@ -11,6 +11,7 @@
 CENTRE = 7.5
 SCALE = 0.25
 CHUNKS = 4
+EARLY = 3
 MESH = pl.DeviceIdType.MESH
 HIGH = lax.Precision.HIGHEST
 
@@ -27,8 +28,8 @@
 
 def kernel(
     r_ref, d_ref, out_ref, hess_ref,
-    k0, k1, k2, k3, diag, ret1, ret2, ys, yh, acc, mine, slots1, part, slots2, splat,
-    x_s, x_r, d_s, d_r, z_s, z_r, y_s, y_r, b_s, b_r, g1_s, g1_r, g2_s, g2_r,
+    k0, k1, k2, k3, diag, ret1, ret2, held, ys, yh, acc, mine, slots1, part, slots2, splat,
+    x_s, x_r, d_s, d_r, z_s, z_r, y_s, y_r, b_s, b_r, l_s, l_r, g1_s, g1_r, g2_s, g2_r,
 ):
     blk, lay, rows, nx = r_ref.shape
     half, group_lay = rows // 2, 2 * lay
@@ -129,12 +130,23 @@
             (partner, gy),
         ).wait_recv()
 
-    def back_copy(j, ch):
+    early = ret1.shape[2]
+    late = half - early
+
+    def back_copy(j, ch, layer):
         vs = pl.ds(ch * vc, vc)
         dst = (ret1, ret2)[j - 1]
         return remote(
-            basis[j].at[vs, pl.ds(1 + theirs_at, lay)], dst.at[vs],
-            b_s.at[j - 1, ch], b_r.at[j - 1, ch], (partner, gy),
+            basis[j].at[vs, pl.ds(1 + theirs_at + layer, 1), pl.ds(0, early)],
+            dst.at[vs, pl.ds(layer, 1)],
+            b_s.at[j - 1, layer, ch], b_r.at[j - 1, layer, ch], (partner, gy),
+        )
+
+    def late_copy(layer):
+        return remote(
+            held.at[:, pl.ds(layer, 1)],
+            out_ref.at[:, pl.ds(layer, 1), pl.ds(pl.multiple_of(hs + early, 8), late)],
+            l_s.at[layer], l_r.at[layer], (partner, gy),
         )
 
     diag_copy = remote(
@@ -315,7 +327,15 @@
                     z_copy(j + 1, ch, 1).start()
 
                 start_rows(j + 1, ch)
-                back_copy(j + 1, ch).start()
+            if j == 0:
+                for layer in range(lay // 2):
+                    back_copy(1, ch, layer).start()
+            elif j == 1:
+                for layer in range(lay // 2, lay):
+                    back_copy(1, ch, layer).start()
+            else:
+                for layer in range(lay):
+                    back_copy(2, ch, layer).start()
 
         chunks(apply)
         gram(2 * j + 1, src, dst, 1, shift, group_lay, half)
@@ -410,11 +430,11 @@
                 normal[k:k + 1, small + u:small + u + 1], (8, 128)
             )
 
-    tiles = half // 8
-
-    def combine(row_start, sources):
+    def combine(dst, layers, row_start, height, sources):
+        tiles = height // 8
+
         def run(i, carry):
-            layer, t = i // tiles, i % tiles
+            layer, t = layers[0] + i // tiles, i % tiles
             at = pl.multiple_of(row_start + t * 8, 8)
             for lane_at in range(lanes):
                 cols = pl.ds(lane_at * 128, 128)
@@ -426,19 +446,32 @@
                     total = splat[u] * vals[0]
                     for k in range(1, small):
                         total = total + splat[k * blk + u] * vals[k]
-                    out_ref[u, layer, pl.ds(at, 8), cols] = total
+                    dst[u, layer, pl.ds(at, 8), cols] = total
             return carry
 
-        lax.fori_loop(0, lay * tiles, run, 0)
-
-    combine(hs, ((r_ref, 0, hs), (k1, 1 + mine_at, 0), (k2, 1 + mine_at, 0)))
+        lax.fori_loop(0, (layers[1] - layers[0]) * tiles, run, 0)
+
+    for layer in range(lay):
+        combine(held, (layer, layer + 1), 0, late, [(k, 1 + theirs_at, early) for k in basis[:ITERS]])
+        late_copy(layer).start()
+    combine(
+        out_ref, (0, lay), hs, half, ((r_ref, 0, hs), (k1, 1 + mine_at, 0), (k2, 1 + mine_at, 0))
+    )
 
     def back_wait(ch):
         for j in (1, 2):
-            back_copy(j, ch).wait()
+            for layer in range(lay):
+                back_copy(j, ch, layer).wait()
 
     chunks(back_wait)
-    combine(os, ((r_ref, 0, os), (ret1, 0, 0), (ret2, 0, 0)))
+    combine(out_ref, (0, lay), os, early, ((r_ref, 0, os), (ret1, 0, 0), (ret2, 0, 0)))
+    for layer in range(lay):
+        late_copy(layer).wait_send()
+        remote(
+            held.at[:, pl.ds(layer, 1)],
+            out_ref.at[:, pl.ds(layer, 1), pl.ds(pl.multiple_of(os + early, 8), late)],
+            l_s.at[layer], l_r.at[layer], (partner, gy),
+        ).wait_recv()
 
     def drain(ch):
         for which in (0, 1):
@@ -467,6 +500,7 @@
 def body(right_side, diagonal):
     blk, lay, rows, nx = right_side.shape
     half, group_lay = rows // 2, 2 * lay
+    early = half * EARLY // 32 * 8
     n_z, n_y = lax.axis_size("gz"), lax.axis_size("gy")
     vmem = lambda *shape: pltpu.VMEM(shape, jnp.float32)
     dma = lambda *shape: pltpu.SemaphoreType.DMA(shape)
@@ -485,8 +519,9 @@
             vmem(blk, group_lay + 2, half, nx),
             vmem(blk, group_lay, half, nx),
             vmem(group_lay, half, nx),
-            vmem(blk, lay, half, nx),
-            vmem(blk, lay, half, nx),
+            vmem(blk, lay, early, nx),
+            vmem(blk, lay, early, nx),
+            vmem(blk, lay, half - early, nx),
             vmem(ITERS, 2, blk, group_lay, nx),
             vmem(ITERS, 2, blk, group_lay, nx),
             vmem(8 * blk * blk, 128),
@@ -499,7 +534,7 @@
             pltpu.SemaphoreType.DMA, pltpu.SemaphoreType.DMA,
             dma(ITERS, 2, CHUNKS), dma(ITERS, 2, CHUNKS),
             dma(ITERS, 2, CHUNKS), dma(ITERS, 2, CHUNKS),
-            dma(2, CHUNKS), dma(2, CHUNKS),
+            dma(2, lay, CHUNKS), dma(2, lay, CHUNKS), dma(lay), dma(lay),
             dma(n_y), dma(n_y), dma(n_z), dma(n_z),
         ],
         compiler_params=pltpu.CompilerParams(

time: 104 us -> 89.4 us (0.86)
  Pallas kernels: 99.5 us -> 84.8 us
    pallas_call x1, Pallas kernels: 99.5 us -> 84.8 us  [body(): pl.pallas_call(kernel, out_shape=(jax.ShapeDtypeStruct(right_side.shape,...]
where the time goes in v2:
time: 89.4 us; the launch traced here: 89.2 us
  Pallas kernels  84.8 us (95%)
  local copies, waits for them, and re-layouts  3.75 us (4%)
    pallas_call x1, Pallas kernels, body(): pl.pallas_call(kernel, out_shape=(jax.ShapeDtypeStruct(right_side.shape,...  84.8 us
    unnamed x4, local copies, waits for them, and re-layouts  3.75 us

profile of v2, /device:TPU:0, one launch (start us, length us, event | category | flops | bytes accessed | tf_op | source)
XLA Modules:
  0.0 89.2 jit_solution(3501788388570530835)
XLA Ops:
  0.6 84.8 %gmres.1 = (f32[8,2,64,512]{3,2,1,0:T(8,128)}, f32[24,32]{1,0:T(8,128)}) custom-call(f32[8,2,64,512]{3,2,1,0:T(8,128)} %r_ref.1, f32[2,64,512]{2,1,0:T(8,128)} %d_ref.1), custom_call_target="tpu_custom_call" | custom-call | tf_op jit(solution)/shard_map/gmres/pallas_call | solution.py:508
  85.5 0.0 copy-start
  85.5 3.1 %copy.6 = f32[8,2,64,512]{3,2,1,0:T(8,128)} copy(f32[8,2,64,512]{3,2,1,0:T(8,128)} %get-tuple-element.4) | data formatting | bytes 4194304
  88.6 0.0 copy-done
  88.6 0.6 copy.7
Async XLA Ops:
  85.5 3.2 %copy-start = (f32[24,32]{1,0:T(8,128)S(1)}, f32[24,32]{1,0:T(8,128)}, u32[]{:S(2)}) copy-start(f32[24,32]{1,0:T(8,128)} %get-tuple-element.5) | copy-start | bytes 9220

commit v3 on v2

--- a/solution.py
+++ b/solution.py
@@ -10,8 +10,9 @@
 ITERS = 3
 CENTRE = 7.5
 SCALE = 0.25
-CHUNKS = 4
-EARLY = 3
+CHUNKS = 8
+AHEAD = 2
+EARLY = 2
 MESH = pl.DeviceIdType.MESH
 HIGH = lax.Precision.HIGHEST
 
@@ -162,6 +163,7 @@
 
     def first(ch):
         exchange(0, ch).start()
+        exchange(1, ch).start()
 
         @pl.when((p == 0) & below)
         def _():
@@ -171,9 +173,10 @@
         def _():
             z_from_rhs(ch, 1).start()
 
-    chunks(first)
-    chunks(lambda ch: exchange(1, ch).start())
+    first(0)
     diag_copy.start()
+    for ch in range(1, AHEAD):
+        first(ch)
 
     def own(v, carry):
         k0[v, pl.ds(1 + mine_at, lay)] = r_ref[v, :, pl.ds(hs, half)]
@@ -228,8 +231,6 @@
         def _():
             z_copy(0, ch, 0).start()
 
-    chunks(relay)
-
     def stage_rows(j, v, layer, value):
         ys[j, 0, v, layer:layer + 1] = value[:1]
         ys[j, 1, v, layer:layer + 1] = value[half - 1:]
@@ -258,19 +259,19 @@
         lax.fori_loop(ch * vc, (ch + 1) * vc, run, 0)
         start_rows(0, ch)
 
-    chunks(arrived)
-    remote(
-        d_ref.at[:, pl.ds(os, half)], diag.at[pl.ds(theirs_at, lay)], d_s, d_r, (partner, gy)
-    ).wait_recv()
+    def diag_arrived():
+        remote(
+            d_ref.at[:, pl.ds(os, half)], diag.at[pl.ds(theirs_at, lay)], d_s, d_r, (partner, gy)
+        ).wait_recv()
 
     row_at = lax.broadcasted_iota(jnp.int32, (half, nx), 0)
     col_at = lax.broadcasted_iota(jnp.int32, (half, nx), 1)
 
-    def step(j):
+    def apply(j, ch):
         src, dst = basis[j], basis[j + 1]
         shift = 0 if j == 2 else 1
 
-        def apply(ch):
+        if True:
             @pl.when(below)
             def _():
                 vs = pl.ds(ch * vc, vc)
@@ -327,22 +328,44 @@
                     z_copy(j + 1, ch, 1).start()
 
                 start_rows(j + 1, ch)
-            if j == 0:
-                for layer in range(lay // 2):
-                    back_copy(1, ch, layer).start()
-            elif j == 1:
-                for layer in range(lay // 2, lay):
-                    back_copy(1, ch, layer).start()
-            else:
-                for layer in range(lay):
-                    back_copy(2, ch, layer).start()
-
-        chunks(apply)
-        gram(2 * j + 1, src, dst, 1, shift, group_lay, half)
-        gram(2 * j + 2, dst, dst, shift, shift, group_lay, half)
-
-    for j in range(ITERS):
-        step(j)
+
+    def grams(j):
+        shift = 0 if j == 2 else 1
+        gram(2 * j + 1, basis[j], basis[j + 1], 1, shift, group_lay, half)
+        gram(2 * j + 2, basis[j + 1], basis[j + 1], shift, shift, group_lay, half)
+
+    def wave(w):
+        relay(w)
+        arrived(w)
+
+        @pl.when(w + AHEAD < CHUNKS)
+        def _():
+            first(w + AHEAD)
+
+        pl.when(w == 1)(diag_arrived)
+        for j in range(ITERS):
+            @pl.when(w >= j + 1)
+            def _():
+                apply(j, w - j - 1)
+
+    def back(j, low, high, layer):
+        def run(ch, carry):
+            back_copy(j, ch, layer).start()
+            return carry
+
+        lax.fori_loop(low, high, run, 0)
+
+    chunks(wave)
+    for tail in range(ITERS):
+        for j in range(tail, ITERS):
+            apply(j, CHUNKS - 1 + tail - j)
+        if tail == 0:
+            back(1, 0, CHUNKS // 2, 0)
+        if tail == 1:
+            back(1, CHUNKS // 2, CHUNKS, 0)
+            for layer in range(1, lay):
+                back(1, 0, CHUNKS, layer)
+        grams(tail)
 
     count = acc.shape[0]
     sums = nt_dot(jnp.ones((8, 128), jnp.float32), acc[...])
@@ -361,6 +384,9 @@
         for off in range(1, n):
             to = (me + off) % n
             remote(src, slots.at[me], send.at[to], recv.at[me], at(to)).start()
+        if axis == "gz":
+            for layer in range(lay):
+                back(2, 0, CHUNKS, layer)
         for off in range(1, n):
             frm = (me + off) % n
             remote(src, slots.at[frm], send.at[frm], recv.at[frm], at(frm)).wait()

time: 89.4 us -> 93.5 us (1.046)
  Pallas kernels: 84.8 us -> 88.9 us
    pallas_call x1, Pallas kernels: 84.8 us -> 88.9 us  [body(): pl.pallas_call(kernel, out_shape=(jax.ShapeDtypeStruct(right_side.shape,...]
where the time goes in v3:
time: 93.5 us; the launch traced here: 93.3 us
  Pallas kernels  88.9 us (95%)
  local copies, waits for them, and re-layouts  3.75 us (4%)
    pallas_call x1, Pallas kernels, body(): pl.pallas_call(kernel, out_shape=(jax.ShapeDtypeStruct(right_side.shape,...  88.9 us
    unnamed x4, local copies, waits for them, and re-layouts  3.75 us

profile of v3, /device:TPU:0, one launch (start us, length us, event | category | flops | bytes accessed | tf_op | source)
XLA Modules:
  0.0 93.3 jit_solution(900046787743663579)
XLA Ops:
  0.6 88.9 %gmres.1 = (f32[8,2,64,512]{3,2,1,0:T(8,128)}, f32[24,32]{1,0:T(8,128)}) custom-call(f32[8,2,64,512]{3,2,1,0:T(8,128)} %r_ref.1, f32[2,64,512]{2,1,0:T(8,128)} %d_ref.1), custom_call_target="tpu_custom_call" | custom-call | tf_op jit(solution)/shard_map/gmres/pallas_call | solution.py:534
  89.6 0.0 copy-start
  89.6 3.1 %copy.6 = f32[8,2,64,512]{3,2,1,0:T(8,128)} copy(f32[8,2,64,512]{3,2,1,0:T(8,128)} %get-tuple-element.4) | data formatting | bytes 4194304
  92.7 0.0 copy-done
  92.7 0.6 copy.7
Async XLA Ops:
  89.6 3.2 %copy-start = (f32[24,32]{1,0:T(8,128)S(1)}, f32[24,32]{1,0:T(8,128)}, u32[]{:S(2)}) copy-start(f32[24,32]{1,0:T(8,128)} %get-tuple-element.5) | copy-start | bytes 9220
